TPU v7x, 256 devices: a whole 4x4x8 slice. The times are simulated.
256 devices in a mesh: dp: 8 (over x, core), vocab: 32 (over z, y).
Axes of the slice: x: 4, y: 4, z: 8, core: 2. Of those that a mesh axis runs over, the one named last changes fastest.
Arguments:
- hidden: bfloat16 [1024, 8192], P(('dp', 'vocab')), may hold values from -350 to 350
- lm_head: bfloat16 [8192, 128256], P(None, ('dp', 'vocab')), may hold values from -0.0625 to 0.0625
- targets: int32 [1024], P(('dp', 'vocab')), may hold values from 0 to 128255
- segment: int32 [1024], P(('dp', 'vocab')), may hold values from 0 to 256, as said below
- pad_mask: int32 [1024], P(('dp', 'vocab')), may hold values from 0 to 1, as said below
- seq_bench: int32 [257], replicated, may hold values from 0 to 7
Outputs:
- token_nll: float32 [1024], P(('dp', 'vocab'))
- bench_total: float32 [8], replicated
- bench_count: float32 [8], replicated
Inputs may be any that keep to these rules, and one draw needn't show every extreme that they name: `segment`: sequence numbers never fall along the pack; each aligned block of 4 tokens holds exactly one place inside it where the number rises by one, and the number does not change between one block's last token and the next block's first. `pad_mask`: the last token of each aligned block of 4 tokens is real.
All inputs are finite; a program needn't handle non-finite values.
Results may differ from a plain program's by a relative error of at most 0.0003.
Values may be sent and summed in bfloat16 or wider, within the bound.
A program may use at most 128 MiB of HBM per device.

v0:
```python
from functools import partial
import functools
import jax
import jax.numpy as jnp
from jax import lax
from jax.sharding import Mesh
from jax.sharding import PartitionSpec as P

NBENCH = 8
DP_VOCAB = ("dp_0", "dp_1", "vocab_0", "vocab_1")
VOCAB = ("vocab_0", "vocab_1")
DP = ("dp_0", "dp_1")


def laid_out(pieces, dim):
    pieces = jnp.moveaxis(pieces, 0, dim)
    shape = pieces.shape
    return pieces.reshape(*shape[:dim], shape[dim] * shape[dim + 1], *shape[dim + 2 :])


def gather_in_order(value, axes, sequence):
    pieces = value
    for k in sequence:
        pieces = lax.all_gather(pieces, axes[k])
    done = sequence[::-1]
    back = [done.index(k) for k in range(len(axes))]
    pieces = pieces.transpose(*back, *range(len(axes), pieces.ndim))
    return pieces.reshape(-1, *value.shape)


def gathered_by_axis(value, axes, sequence, dim):
    return laid_out(gather_in_order(value, axes, sequence), dim)


def whole_of(value, axes, dim):
    out = value
    for number in range(len(axes) - 1, -1, -1):
        out = lax.all_gather(out, axes[number], axis=dim, tiled=True)
    return out


def gathered_once(value, axis):
    leaves = jax.tree.leaves(value)
    sequence = sorted(range(len(leaves)), key=lambda k: -leaves[k].size)
    width = (1, *leaves[sequence[0]].shape)[-1]
    lines = [
        jnp.pad(leaves[k].reshape(-1), (0, -leaves[k].size % width)).reshape(-1, width)
        for k in sequence
    ]
    both, at, found = (lax.all_gather(jnp.concatenate(lines), axis), 0, {})
    for k, line in zip(sequence, lines):
        share = both[:, at : at + len(line)].reshape(len(both), -1)
        found[k] = share[:, : leaves[k].size].reshape(-1, *leaves[k].shape)
        at += len(line)
    numbers = iter(range(len(leaves)))
    return jax.tree.map(lambda _: found[next(numbers)], value)


def merged_by_axis(value, axes, combine):
    for axis in axes:
        pieces = gathered_once(value, axis)
        value = jax.tree.map(lambda part: part[0], pieces)
        for k in range(1, lax.axis_size(axis)):
            value = combine(value, jax.tree.map(lambda part: part[k], pieces))
    return value


def from_behind(value, axis, steps):
    count = lax.axis_size(axis)
    leading, last = (max(0, -steps), min(count, count - steps))
    return lax.ppermute(value, axis, [(source, source + steps) for source in range(leading, last)])


def one_axis_at_a_time(value, axes):
    return functools.reduce(lax.psum, axes, value)


def shard_stats(piece, start, lm_head, all_targets, col_start):
    logits = jnp.dot(piece, lm_head, preferred_element_type=jnp.float32)
    row_top = jnp.max(logits, axis=1)
    expsum = jnp.sum(jnp.exp(logits - row_top[:, None]), axis=1)
    wanted = all_targets - col_start
    columns = lax.broadcasted_iota(jnp.int32, logits.shape, 1)
    picked = jnp.sum(jnp.where(columns == wanted[:, None], logits, 0.0), axis=1)
    return jnp.stack([row_top, expsum, picked], axis=0)


def merge_rows(first, second):
    top = jnp.maximum(first[0], second[0])
    total = first[1] * jnp.exp(first[0] - top) + second[1] * jnp.exp(second[0] - top)
    return (top, total, first[2] + second[2])


def body(hidden, lm_head, targets, segment, pad_mask, seq_bench):
    tok_dev = hidden.shape[0]
    voc_dev = lm_head.shape[1]
    own_index = lax.axis_index(DP_VOCAB)
    col_start = own_index * voc_dev
    row_start = own_index * tok_dev
    all_targets = gathered_by_axis(targets, DP_VOCAB, (0, 2, 3, 1), 0)
    per_piece = partial(shard_stats, lm_head=lm_head, all_targets=all_targets, col_start=col_start)
    group_rows = whole_of(hidden, VOCAB, 0)
    stats = per_piece(lax.all_gather(group_rows, DP, axis=0, tiled=True), jnp.int32(0))
    top_all, total_all, picked_all = merged_by_axis(
        (stats[0], stats[1], stats[2]), DP_VOCAB, merge_rows
    )
    top = lax.dynamic_slice_in_dim(top_all, row_start, tok_dev, 0)
    total = lax.dynamic_slice_in_dim(total_all, row_start, tok_dev, 0)
    picked = lax.dynamic_slice_in_dim(picked_all, row_start, tok_dev, 0)
    token_nll = top + jnp.log(total) - picked
    next_first = from_behind(segment[:1] + 1, DP_VOCAB, -1)
    following = jnp.concatenate([segment[1:] + 1, next_first])
    keep = (pad_mask * (segment + 1 == following).astype(jnp.int32)).astype(jnp.float32)
    seq_count = seq_bench.shape[0]
    seq_hot = segment[:, None] == lax.broadcasted_iota(jnp.int32, (1, seq_count), 1)
    bench_of = jnp.sum(jnp.where(seq_hot, seq_bench[None, :], 0), axis=1)
    bench_hot = (bench_of[:, None] == lax.broadcasted_iota(jnp.int32, (1, NBENCH), 1)).astype(
        jnp.float32
    )
    weighted = keep * token_nll
    bench_total, bench_count = (
        one_axis_at_a_time(jnp.sum(bench_hot * weighted[:, None], axis=0), DP_VOCAB),
        one_axis_at_a_time(jnp.sum(bench_hot * keep[:, None], axis=0), DP_VOCAB),
    )
    return (token_nll, bench_total, bench_count)


def solution(mesh):
    split = Mesh(mesh.devices.reshape(4, 2, 8, 4), ("dp_0", "dp_1", "vocab_0", "vocab_1"))
    return jax.shard_map(
        body,
        mesh=split,
        in_specs=(P(DP_VOCAB, None), P(None, DP_VOCAB), P(DP_VOCAB), P(DP_VOCAB), P(DP_VOCAB), P()),
        out_specs=(P(DP_VOCAB), P(), P()),
        check_vma=False,
    )
```

profile of v0, /device:TPU:2, one launch (start us, length us, event | category | flops | bytes accessed | tf_op | source)
XLA Modules:
  0.0 264.9 jit_solution(8159874351671681301)
XLA Ops:
  7.2 0.0 copy-start.4
  7.2 0.0 copy-start
  7.2 0.0 copy-start.3
  7.2 0.0 copy-start.1
  7.2 0.0 all-gather.17.cloned.1.call-start
  7.3 13.0 %all-gather.8 = bf16[4,4,8192]{2,1,0:T(4,128)(2,1)S(1)} all-gather(bf16[1,4,8192]{2,1,0:T(4,128)(2,1)} %bitcast.295), channel_id=1, replica_groups=mesh['dp_0'=4,'dp_1'=2,'vocab_0'=8,'vocab_1'=4] {'vocab_1'}, dimensions={0}, use_global_device_ids=true | all-gather | bytes 327680 | tf_op jit(solution)/shard_map/all_gather | solution.py:38
  20.2 0.8 reshape.920
  21.0 0.0 all-gather.17.cloned.1.call-update
  21.0 0.0 all-gather.19.cloned.1.call-start
  21.1 43.2 %all-gather.17.cloned.1.call-done = bf16[128,8192]{1,0:T(8,128)(2,1)} async-done(((bf16[16,8192]{1,0:T(8,128)(2,1)}), bf16[128,8192]{1,0:T(8,128)(2,1)}) %all-gather.17.cloned.1.call-update) | async-done | bytes 2097168 | tf_op jit(solution)/shard_map/all_gather | solution.py:38
  64.3 0.0 all-gather.19.cloned.1.call-update
  64.3 0.0 copy-done
  64.4 3.2 %collective-permute-start = (s32[1]{0:T(128)}, s32[1]{0:T(128)}, u32[]{:S(2)}, u32[]{:S(2)}) collective-permute-start(s32[1]{0:T(128)} %add.335), channel_id=1, source_target_pairs={{1,0},{2,1},{3,2},{4,3},{5,4},{6,5},{7,6},{8,7},{9,8},{10,9},{11,1... | collective-permute-start | bytes 20 | tf_op jit(solution)/shard_map/ppermute | solution.py:71
  67.6 0.0 copy-done.4
  67.6 0.6 dynamic-slice.1
  68.8 0.0 copy-done.3
  68.9 0.2 dynamic-update-slice
  69.1 7.9 %all-reduce = s32[16]{0:T(128)S(1)} all-reduce(s32[16]{0:T(128)S(1)} %dynamic-update-slice), channel_id=2, replica_groups=mesh['dp_0'=4,'dp_1'=2,'vocab_0'=8,'vocab_1'=4] {'dp_0'}, use_global_device_ids=true, to_apply=%add | all-reduce | flops 16 | bytes 128
  77.0 0.1 reshape.921
  77.1 26.0 %all-gather.9 = s32[8,4,4]{2,1,0:T(4,128)S(1)} all-gather(s32[1,4,4]{2,1,0:T(4,128)S(1)} %reshape.921), channel_id=3, replica_groups=mesh['dp_0'=4,'dp_1'=2,'vocab_0'=8,'vocab_1'=4] {'vocab_0'}, dimensions={0}, use_global_device_ids=true | all-gather | bytes 576 | tf_op jit(solution)/shard_map/all_gather | solution.py:24
  103.2 11.9 %all-gather.2 = s32[32,4,4]{2,1,0:T(4,128)S(1)} all-gather(s32[8,4,4]{2,1,0:T(4,128)S(1)} %all-gather.9), channel_id=4, replica_groups=mesh['dp_0'=4,'dp_1'=2,'vocab_0'=8,'vocab_1'=4] {'vocab_1'}, dimensions={0}, use_global_device_ids=true | all-gather | bytes 2560 | tf_op jit(solution)/shard_map/all_gather | solution.py:24
  115.0 0.2 copy.14
  115.2 1.9 all-gather.3
  117.1 0.3 copy.16
  117.3 0.2 sub.270
  117.5 0.0 copy-done.1
  117.5 0.2 select_reduce_fusion.1
  117.7 0.1 slice_add_fusion.11
  117.8 34.1 %all-gather.19.cloned.1.call-done = bf16[1024,8192]{1,0:T(8,128)(2,1)} async-done(((bf16[128,8192]{1,0:T(8,128)(2,1)}), bf16[1024,8192]{1,0:T(8,128)(2,1)}) %all-gather.19.cloned.1.call-update) | async-done | bytes 16777232 | tf_op jit(solution)/shard_map/all_gather | solution.py:103
  151.8 14.3 %fusion.61 = (f32[1024]{0:T(1024)S(1)}, f32[1024,501]{0,1:T(8,128)S(1)}) fusion(bf16[1024,8192]{1,0:T(8,128)(2,1)} %all-gather.19.cloned.1.call-done, bf16[8192,501]{0,1:T(8,128)(2,1)} %param.7), kind=kOutput, calls=%fused_computation.115 | convolution fusion | flops 8405897216 | bytes 27041792 | tf_op jit(solution)/shard_map/dot_general | solution.py:79
  166.2 0.0 copy-start.2
  166.2 0.5 exponential_reduce_fusion
  166.7 10.7 %all-gather.10 = f32[4,3,1024]{2,1,0:T(4,128)S(1)} all-gather(f32[1,3,1024]{2,1,0:T(4,128)S(1)} %maximum_bitcast_fusion), channel_id=6, replica_groups=mesh['dp_0'=4,'dp_1'=2,'vocab_0'=8,'vocab_1'=4] {'dp_0'}, dimensions={0}, use_global_device_ids=true | all-gather | bytes 61440 | tf_op jit(solution)/shard_map/all_gather | solution.py:50
  177.5 0.1 fusion.28
  177.6 1.8 all-gather.11
  179.5 26.3 %all-gather.12 = f32[8,3,1024]{2,1,0:T(4,128)S(1)} all-gather(f32[1,3,1024]{2,1,0:T(4,128)S(1)} %maximum_bitcast_fusion.2), channel_id=8, replica_groups=mesh['dp_0'=4,'dp_1'=2,'vocab_0'=8,'vocab_1'=4] {'vocab_0'}, dimensions={0}, use_global_device_ids=true | all-gather | bytes 110592 | tf_op jit(solution)/shard_map/all_gather | solution.py:50
  205.8 0.1 fusion.2
  205.9 12.2 %all-gather.13 = f32[4,3,1024]{2,1,0:T(4,128)S(1)} all-gather(f32[1,3,1024]{2,1,0:T(4,128)S(1)} %maximum_bitcast_fusion.3), channel_id=9, replica_groups=mesh['dp_0'=4,'dp_1'=2,'vocab_0'=8,'vocab_1'=4] {'vocab_1'}, dimensions={0}, use_global_device_ids=true | all-gather | bytes 61440 | tf_op jit(solution)/shard_map/all_gather | solution.py:50
  218.2 0.0 collective-permute-done
  218.2 0.0 copy-done.2
  218.2 1.2 fusion.53
  219.5 0.1 select_reduce_fusion.2
  219.5 9.6 %all-reduce.3 = (f32[8]{0:T(128)S(1)}, f32[8]{0:T(128)S(1)}) all-reduce(f32[8]{0:T(128)S(1)} %get-tuple-element.6, f32[8]{0:T(128)S(1)} %get-tuple-element.5), channel_id=1, replica_groups=mesh['dp_0'=4,'dp_1'=2,'vocab_0'=8,'vocab_1'=4] {'dp_0'}, use_global_device_ids=true, to_apply=%region_5.6 | all-reduce | flops 16 | bytes 128 | tf_op jit(solution)/shard_map/psum | solution.py:75
  229.1 2.5 all-reduce.4
  231.5 15.9 %all-reduce.1 = (f32[8]{0:T(128)S(1)}, f32[8]{0:T(128)S(1)}) all-reduce(f32[8]{0:T(128)S(1)} %get-tuple-element.13, f32[8]{0:T(128)S(1)} %get-tuple-element.14), channel_id=1, replica_groups=mesh['dp_0'=4,'dp_1'=2,'vocab_0'=8,'vocab_1'=4] {'vocab_0'}, use_global_device_ids=true, to_apply=%region_7.8 | all-reduce | flops 16 | bytes 128 | tf_op jit(solution)/shard_map/psum | solution.py:75
  247.5 10.6 %all-reduce.2 = (f32[8]{0:T(128)}, f32[8]{0:T(128)}) all-reduce(f32[8]{0:T(128)S(1)} %get-tuple-element.7, f32[8]{0:T(128)S(1)} %get-tuple-element.8), channel_id=1, replica_groups=mesh['dp_0'=4,'dp_1'=2,'vocab_0'=8,'vocab_1'=4] {'vocab_1'}, use_global_device_ids=true, to_apply=%region_8.9 | all-reduce | flops 16 | bytes 128 | tf_op jit(solution)/shard_map/psum | solution.py:75
  (13 shorter events, 0.2 us)
Async XLA Ops:
  7.2 60.4 %copy-start.4 = (u32[256]{0:T(256)S(1)}, u32[256]{0:T(256)}, u32[]{:S(2)}) copy-start(u32[256]{0:T(256)} %constant.51) | copy-start | bytes 3076
  7.2 57.2 %copy-start = (s32[4]{0:T(128)S(1)}, s32[4]{0:T(128)}, u32[]{:S(2)}) copy-start(s32[4]{0:T(128)} %param.9) | copy-start | bytes 52
  7.2 61.7 %copy-start.3 = (s32[4]{0:T(128)S(1)}, s32[4]{0:T(128)}, u32[]{:S(2)}) copy-start(s32[4]{0:T(128)} %param.8) | copy-start | bytes 52
  7.2 110.3 %copy-start.1 = (s32[257]{0:T(512)S(1)}, s32[257]{0:T(512)}, u32[]{:S(2)}) copy-start(s32[257]{0:T(512)} %param.11) | copy-start | bytes 3088
  7.2 57.1 %all-gather.17.cloned.1.call-start = ((), (), s32[]{:S(2)}) async-start(), calls=%async_computation | async-start | bytes 2359296 | tf_op jit(solution)/shard_map/all_gather | solution.py:38
  21.0 130.8 %all-gather.19.cloned.1.call-start = ((), (), s32[]{:S(2)}) async-start(), calls=%async_computation.1 | async-start | bytes 18874368 | tf_op jit(solution)/shard_map/all_gather | solution.py:103
  64.4 153.8 %collective-permute-start = (s32[1]{0:T(128)}, s32[1]{0:T(128)}, u32[]{:S(2)}, u32[]{:S(2)}) collective-permute-start(s32[1]{0:T(128)} %add.335), channel_id=1, source_target_pairs={{1,0},{2,1},{3,2},{4,3},{5,4},{6,5},{7,6},{8,7},{9,8},{10,9},{11,1... | collective-permute-start | bytes 20 | tf_op jit(solution)/shard_map/ppermute | solution.py:71
  166.2 52.1 %copy-start.2 = (s32[4]{0:T(128)S(1)}, s32[4]{0:T(128)}, u32[]{:S(2)}) copy-start(s32[4]{0:T(128)} %param.10) | copy-start | bytes 52
Sparse Core Ops, SparseCore 0:
  21.1 43.1 all-gather.16
  66.2 85.6 all-gather.18
where the time goes:
time: 265 us
  blocking collectives  150 us (57%)
  waiting for transfers between devices  77.4 us (29%)
  between operations  14.9 us (6%)
  matrix products  14.3 us (5%)
  starting transfers between devices  3.28 us (1%)
    all_gather x4, blocking collectives, gathered_once(): both, at, found = (lax.all_gather(jnp.concatenate(lines), axis), 0, {})  51.1 us
    all_gather x1, waiting for transfers between devices, whole_of(): out = lax.all_gather(out, axes[number], axis=dim, tiled=True)  43.2 us
    all_gather x3, blocking collectives, gather_in_order(): pieces = lax.all_gather(pieces, axes[k])  39.7 us
    psum x4, blocking collectives, one_axis_at_a_time(): return functools.reduce(lax.psum, axes, value)  38.6 us
    all_gather x1, waiting for transfers between devices, body(): lax.all_gather(group_rows, DP, axis=0, tiled=True)  34.1 us
    dot_general x1, matrix products, shard_stats(): logits = jnp.dot(piece, lm_head, preferred_element_type=jnp.float32)  14.3 us
    all_gather x1, blocking collectives, whole_of(): out = lax.all_gather(out, axes[number], axis=dim, tiled=True)  13 us
    unnamed x1, blocking collectives  7.94 us
  transfers between devices with their start and end apart: 3, of which 2 were waited for; matrix products, arithmetic and copies ran while one was open for 6% of the time, Pallas kernels for 0%

commit v1 on v0

--- a/solution.py
+++ b/solution.py
@@ -100,7 +100,13 @@
     all_targets = gathered_by_axis(targets, DP_VOCAB, (0, 2, 3, 1), 0)
     per_piece = partial(shard_stats, lm_head=lm_head, all_targets=all_targets, col_start=col_start)
     group_rows = whole_of(hidden, VOCAB, 0)
-    stats = per_piece(lax.all_gather(group_rows, DP, axis=0, tiled=True), jnp.int32(0))
+
+    def row_store(sample, along_dim):
+        z = lax.all_to_all(jnp.stack(lax.axis_size(DP) * [sample]), DP, 0, 0)
+        aux = jnp.concatenate(z, axis=along_dim)
+        return aux
+
+    stats = per_piece(row_store(group_rows, 0), jnp.int32(0))
     top_all, total_all, picked_all = merged_by_axis(
         (stats[0], stats[1], stats[2]), DP_VOCAB, merge_rows
     )

time: 265 us -> 412 us (1.55)
  blocking collectives: 150 us -> 314 us
  waiting for transfers between devices: 77.4 us -> 43.3 us
  starting transfers between devices: 3.28 us -> 13.4 us
  local copies, waits for them, and re-layouts: 2.32 us -> 9.15 us
    unnamed x1, blocking collectives: 7.94 us -> 177 us
    all_gather x1 -> x0, waiting for transfers between devices: 34.1 us -> none  [body(): lax.all_gather(group_rows, DP, axis=0, tiled=True)]
    another operation x0 -> x1, local copies, waits for them, and re-layouts: none -> 6.84 us  [row_store(): z = lax.all_to_all(jnp.stack(lax.axis_size(DP) * [sample]), DP, 0, 0)]
    all_to_all x0 -> x1, starting transfers between devices: none -> 6.34 us  [row_store(): z = lax.all_to_all(jnp.stack(lax.axis_size(DP) * [sample]), DP, 0, 0)]
    all_gather x3, blocking collectives: 39.7 us -> 35.4 us  [gather_in_order(): pieces = lax.all_gather(pieces, axes[k])]
  transfers between devices with their start and end apart: 3 -> 3, of which waited for: 2 -> 1; matrix products, arithmetic and copies ran while one was open for 6% -> 4% of each run, Pallas kernels for 0% -> 0%
where the time goes in v1:
time: 412 us
  blocking collectives  314 us (76%)
  waiting for transfers between devices  43.3 us (11%)
  between operations  14.9 us (4%)
  matrix products  14.3 us (3%)
  starting transfers between devices  13.4 us (3%)
  local copies, waits for them, and re-layouts  9.15 us (2%)
    unnamed x1, blocking collectives  177 us
    all_gather x4, blocking collectives, gathered_once(): both, at, found = (lax.all_gather(jnp.concatenate(lines), axis), 0, {})  49 us
    all_gather x1, waiting for transfers between devices, whole_of(): out = lax.all_gather(out, axes[number], axis=dim, tiled=True)  43.3 us
    psum x4, blocking collectives, one_axis_at_a_time(): return functools.reduce(lax.psum, axes, value)  39.5 us
    all_gather x3, blocking collectives, gather_in_order(): pieces = lax.all_gather(pieces, axes[k])  35.4 us
    dot_general x1, matrix products, shard_stats(): logits = jnp.dot(piece, lm_head, preferred_element_type=jnp.float32)  14.3 us
    all_gather x1, blocking collectives, whole_of(): out = lax.all_gather(out, axes[number], axis=dim, tiled=True)  13 us
  transfers between devices with their start and end apart: 3, of which 1 were waited for; matrix products, arithmetic and copies ran while one was open for 4% of the time, Pallas kernels for 0%

profile of v1, /device:TPU:2, one launch (start us, length us, event | category | flops | bytes accessed | tf_op | source)
XLA Modules:
  0.0 411.5 jit_solution(11447912467997019309)
XLA Ops:
  7.2 0.0 all-gather.16.cloned.1.call-start
  7.2 13.0 %all-gather.8 = bf16[4,4,8192]{2,1,0:T(4,128)(2,1)S(1)} all-gather(bf16[1,4,8192]{2,1,0:T(4,128)(2,1)} %bitcast.296), channel_id=1, replica_groups=mesh['dp_0'=4,'dp_1'=2,'vocab_0'=8,'vocab_1'=4] {'vocab_1'}, dimensions={0}, use_global_device_ids=true | all-gather | bytes 327680 | tf_op jit(solution)/shard_map/all_gather | solution.py:38
  20.2 0.8 reshape.926
  21.0 0.0 all-gather.16.cloned.1.call-update
  21.0 43.3 %all-gather.16.cloned.1.call-done = bf16[128,8192]{1,0:T(8,128)(2,1)} async-done(((bf16[16,8192]{1,0:T(8,128)(2,1)}), bf16[128,8192]{1,0:T(8,128)(2,1)}) %all-gather.16.cloned.1.call-update) | async-done | bytes 2097168 | tf_op jit(solution)/shard_map/all_gather | solution.py:38
  64.3 6.8 %stack.2 = bf16[8,128,8192]{2,1,0:T(8,128)(2,1)} broadcast(bf16[128,8192]{1,0:T(8,128)(2,1)} %all-gather.16.cloned.1.call-done), dimensions={1,2} | broadcast | bytes 18874368 | tf_op jit(solution)/shard_map/stack | solution.py:105
  71.1 0.0 copy-start
  71.1 0.0 copy-start.4
  71.1 0.0 copy-start.3
  71.1 0.0 copy-start.1
  71.1 6.3 %all-to-all-start = ((bf16[8,128,8192]{2,1,0:T(8,128)(2,1)}), bf16[8,128,8192]{2,1,0:T(8,128)(2,1)}, u32[]{:S(2)}, u32[]{:S(2)}) async-start(bf16[8,128,8192]{2,1,0:T(8,128)(2,1)} %stack.2), calls=%async_computation | async-start | bytes 33554432 | tf_op jit(solution)/shard_map/all_to_all | solution.py:105
  77.5 0.0 copy-done
  77.5 7.0 %collective-permute-start = (s32[1]{0:T(128)}, s32[1]{0:T(128)}, u32[]{:S(2)}, u32[]{:S(2)}) collective-permute-start(s32[1]{0:T(128)} %add.335), channel_id=1, source_target_pairs={{1,0},{2,1},{3,2},{4,3},{5,4},{6,5},{7,6},{8,7},{9,8},{10,9},{11,1... | collective-permute-start | bytes 20 | tf_op jit(solution)/shard_map/ppermute | solution.py:71
  84.5 0.0 copy-done.4
  84.5 0.6 dynamic-slice.1
  85.8 0.0 copy-done.3
  85.8 0.2 dynamic-update-slice
  86.0 177.1 %all-reduce = s32[16]{0:T(128)S(1)} all-reduce(s32[16]{0:T(128)S(1)} %dynamic-update-slice), channel_id=2, replica_groups=mesh['dp_0'=4,'dp_1'=2,'vocab_0'=8,'vocab_1'=4] {'dp_0'}, use_global_device_ids=true, to_apply=%add | all-reduce | flops 16 | bytes 128
  263.1 0.1 reshape.927
  263.1 21.4 %all-gather.9 = s32[8,4,4]{2,1,0:T(4,128)S(1)} all-gather(s32[1,4,4]{2,1,0:T(4,128)S(1)} %reshape.927), channel_id=3, replica_groups=mesh['dp_0'=4,'dp_1'=2,'vocab_0'=8,'vocab_1'=4] {'vocab_0'}, dimensions={0}, use_global_device_ids=true | all-gather | bytes 576 | tf_op jit(solution)/shard_map/all_gather | solution.py:24
  284.5 12.2 %all-gather.2 = s32[32,4,4]{2,1,0:T(4,128)S(1)} all-gather(s32[8,4,4]{2,1,0:T(4,128)S(1)} %all-gather.9), channel_id=4, replica_groups=mesh['dp_0'=4,'dp_1'=2,'vocab_0'=8,'vocab_1'=4] {'vocab_1'}, dimensions={0}, use_global_device_ids=true | all-gather | bytes 2560 | tf_op jit(solution)/shard_map/all_gather | solution.py:24
  296.7 0.2 copy.14
  296.9 1.9 all-gather.3
  298.8 0.3 copy.16
  299.0 0.2 sub.270
  299.2 0.0 copy-done.1
  299.2 0.2 select_reduce_fusion.1
  299.4 0.1 slice_add_fusion.11
  299.4 0.0 all-to-all-done
  299.4 14.3 %fusion.61 = (f32[1024]{0:T(1024)S(1)}, f32[1024,501]{0,1:T(8,128)S(1)}) fusion(bf16[1024,8192]{1,0:T(8,128)(2,1)} %bitcast.1, bf16[8192,501]{0,1:T(8,128)(2,1)} %param.7), kind=kOutput, calls=%fused_computation.115 | convolution fusion | flops 8405897216 | bytes 27041792 | tf_op jit(solution)/shard_map/dot_general | solution.py:79
  313.8 0.0 copy-start.2
  313.8 0.5 exponential_reduce_fusion
  314.4 10.8 %all-gather.10 = f32[4,3,1024]{2,1,0:T(4,128)S(1)} all-gather(f32[1,3,1024]{2,1,0:T(4,128)S(1)} %maximum_bitcast_fusion), channel_id=6, replica_groups=mesh['dp_0'=4,'dp_1'=2,'vocab_0'=8,'vocab_1'=4] {'dp_0'}, dimensions={0}, use_global_device_ids=true | all-gather | bytes 61440 | tf_op jit(solution)/shard_map/all_gather | solution.py:50
  325.1 0.1 fusion.28
  325.2 1.8 all-gather.11
  327.1 24.6 %all-gather.12 = f32[8,3,1024]{2,1,0:T(4,128)S(1)} all-gather(f32[1,3,1024]{2,1,0:T(4,128)S(1)} %maximum_bitcast_fusion.2), channel_id=8, replica_groups=mesh['dp_0'=4,'dp_1'=2,'vocab_0'=8,'vocab_1'=4] {'vocab_0'}, dimensions={0}, use_global_device_ids=true | all-gather | bytes 110592 | tf_op jit(solution)/shard_map/all_gather | solution.py:50
  351.7 0.1 fusion.2
  351.9 11.9 %all-gather.13 = f32[4,3,1024]{2,1,0:T(4,128)S(1)} all-gather(f32[1,3,1024]{2,1,0:T(4,128)S(1)} %maximum_bitcast_fusion.3), channel_id=9, replica_groups=mesh['dp_0'=4,'dp_1'=2,'vocab_0'=8,'vocab_1'=4] {'vocab_1'}, dimensions={0}, use_global_device_ids=true | all-gather | bytes 61440 | tf_op jit(solution)/shard_map/all_gather | solution.py:50
  363.8 0.0 collective-permute-done
  363.8 0.0 copy-done.2
  363.8 1.3 fusion.53
  365.1 0.1 select_reduce_fusion.2
  365.2 10.6 %all-reduce.3 = (f32[8]{0:T(128)S(1)}, f32[8]{0:T(128)S(1)}) all-reduce(f32[8]{0:T(128)S(1)} %get-tuple-element.6, f32[8]{0:T(128)S(1)} %get-tuple-element.5), channel_id=1, replica_groups=mesh['dp_0'=4,'dp_1'=2,'vocab_0'=8,'vocab_1'=4] {'dp_0'}, use_global_device_ids=true, to_apply=%region_5.6 | all-reduce | flops 16 | bytes 128 | tf_op jit(solution)/shard_map/psum | solution.py:75
  375.8 2.5 all-reduce.4
  378.2 15.8 %all-reduce.1 = (f32[8]{0:T(128)S(1)}, f32[8]{0:T(128)S(1)}) all-reduce(f32[8]{0:T(128)S(1)} %get-tuple-element.13, f32[8]{0:T(128)S(1)} %get-tuple-element.14), channel_id=1, replica_groups=mesh['dp_0'=4,'dp_1'=2,'vocab_0'=8,'vocab_1'=4] {'vocab_0'}, use_global_device_ids=true, to_apply=%region_7.8 | all-reduce | flops 16 | bytes 128 | tf_op jit(solution)/shard_map/psum | solution.py:75
  394.1 10.6 %all-reduce.2 = (f32[8]{0:T(128)}, f32[8]{0:T(128)}) all-reduce(f32[8]{0:T(128)S(1)} %get-tuple-element.7, f32[8]{0:T(128)S(1)} %get-tuple-element.8), channel_id=1, replica_groups=mesh['dp_0'=4,'dp_1'=2,'vocab_0'=8,'vocab_1'=4] {'vocab_1'}, use_global_device_ids=true, to_apply=%region_8.9 | all-reduce | flops 16 | bytes 128 | tf_op jit(solution)/shard_map/psum | solution.py:75
  (13 shorter events, 0.2 us)
Async XLA Ops:
  7.2 57.1 %all-gather.16.cloned.1.call-start = ((), (), s32[]{:S(2)}) async-start(), calls=%async_computation.1 | async-start | bytes 2359296 | tf_op jit(solution)/shard_map/all_gather | solution.py:38
  71.1 6.4 %copy-start = (s32[4]{0:T(128)S(1)}, s32[4]{0:T(128)}, u32[]{:S(2)}) copy-start(s32[4]{0:T(128)} %param.9) | copy-start | bytes 52
  71.1 13.4 %copy-start.4 = (u32[256]{0:T(256)S(1)}, u32[256]{0:T(256)}, u32[]{:S(2)}) copy-start(u32[256]{0:T(256)} %constant.51) | copy-start | bytes 3076
  71.1 14.6 %copy-start.3 = (s32[4]{0:T(128)S(1)}, s32[4]{0:T(128)}, u32[]{:S(2)}) copy-start(s32[4]{0:T(128)} %param.8) | copy-start | bytes 52
  71.1 228.1 %copy-start.1 = (s32[257]{0:T(512)S(1)}, s32[257]{0:T(512)}, u32[]{:S(2)}) copy-start(s32[257]{0:T(512)} %param.11) | copy-start | bytes 3088
  71.1 228.3 %all-to-all-start = ((bf16[8,128,8192]{2,1,0:T(8,128)(2,1)}), bf16[8,128,8192]{2,1,0:T(8,128)(2,1)}, u32[]{:S(2)}, u32[]{:S(2)}) async-start(bf16[8,128,8192]{2,1,0:T(8,128)(2,1)} %stack.2), calls=%async_computation | async-start | bytes 33554432 | tf_op jit(solution)/shard_map/all_to_all | solution.py:105
  77.5 286.3 %collective-permute-start = (s32[1]{0:T(128)}, s32[1]{0:T(128)}, u32[]{:S(2)}, u32[]{:S(2)}) collective-permute-start(s32[1]{0:T(128)} %add.335), channel_id=1, source_target_pairs={{1,0},{2,1},{3,2},{4,3},{5,4},{6,5},{7,6},{8,7},{9,8},{10,9},{11,1... | collective-permute-start | bytes 20 | tf_op jit(solution)/shard_map/ppermute | solution.py:71
  313.8 50.1 %copy-start.2 = (s32[4]{0:T(128)S(1)}, s32[4]{0:T(128)}, u32[]{:S(2)}) copy-start(s32[4]{0:T(128)} %param.10) | copy-start | bytes 52
Sparse Core Ops, SparseCore 0:
  21.1 43.1 all-gather.15
